TPU v7x, 32 devices: a whole 2x2x4 slice. The times are simulated.
32 devices in a mesh: ctx: 16 (over z, x, core), tp: 2 (over y).
Axes of the slice: x: 2, y: 2, z: 4, core: 2. Of those that a mesh axis runs over, the one named last changes fastest.
Arguments:
- queries: bfloat16 [4096, 12288], P(('ctx', 'tp')), may hold values from -64 to 64
- keys: bfloat16 [4096, 1024], P(('ctx', 'tp')), may hold values from -4 to 4
- values: bfloat16 [4096, 1024], P(('ctx', 'tp')), may hold values from -6 to 6
- block_order: int32 [16], replicated, may hold values from 0 to 15, each once
Outputs:
- attended: bfloat16 [4096, 12288], P(('ctx', 'tp'))
Inputs may be any that keep to these rules, and one draw needn't show every extreme that they name: A permutation: block r holds sequence span block_order[r] in its first 128 rows and span 2 * 16 - 1 - block_order[r] in its last 128 rows.
All inputs are finite; a program needn't handle non-finite values.
Results may differ from a plain program's by a relative error of at most 0.003.
Values may be sent and summed in bfloat16 or wider, within the bound.
No kernel may reach another device: no remote copies, remote signals or barrier semaphores. Data moves between devices by JAX's collectives and lax.ppermute only.
A program may use at most 128 MiB of HBM per device.

v0:
```python
import functools
import math

import jax
import jax.numpy as jnp
from jax import lax
from jax.experimental import pallas as pl
from jax.experimental.pallas import tpu as pltpu
from jax.sharding import PartitionSpec as P


HD = 128
PREV = 3


MASKED_SCORE = -1e30


def passed_along(value, axis, steps):
    count = lax.axis_size(axis)
    pairs = [(source, (source + steps) % count) for source in range(count)]
    return lax.ppermute(value, axis, pairs)


def block_positions(block_order, block_index, first_row, count, span_rows):
    block_total = block_order.shape[0]
    leading = jnp.sum(
        jnp.where(jnp.arange(block_total, dtype=jnp.int32) == block_index, block_order, 0)
    )
    row_ids = first_row + jnp.arange(count, dtype=jnp.int32)
    return jnp.where(
        row_ids < span_rows,
        leading * span_rows + row_ids,
        (2 * block_total - 1 - leading) * span_rows + row_ids - span_rows,
    )


def update(carried, queries_h, query_pos, key_part, value_part, key_pos):
    piece_rows = key_part.shape[0]
    block_rows = math.gcd(piece_rows, 256)
    block_count = piece_rows // block_rows
    score_scale = 1.0 / math.sqrt(queries_h.shape[-1])
    key_blocks = key_part.reshape(block_count, block_rows, key_part.shape[1], key_part.shape[2])
    value_blocks = value_part.reshape(
        block_count, block_rows, value_part.shape[1], value_part.shape[2]
    )
    pos_blocks = key_pos.reshape(block_count, block_rows)

    def advance(running, blocks_in):
        running_max, running_sum, numerator = running
        key_block, value_block, pos_block = blocks_in
        scores = (
            jnp.einsum("tkgd,skd->tkgs", queries_h, key_block, preferred_element_type=jnp.float32)
            * score_scale
        )
        visible = pos_block[None, None, None, :] <= query_pos[:, None, None, None]
        block_max = jnp.max(jnp.where(visible, scores, MASKED_SCORE), axis=-1)
        new_max = jnp.maximum(running_max, block_max)
        exp_scores = jnp.where(visible, jnp.exp(scores - new_max[..., None]), 0.0)
        rescale = jnp.exp(running_max - new_max)
        running_sum = running_sum * rescale + jnp.sum(exp_scores, axis=-1)
        weights = exp_scores.astype(jnp.bfloat16)
        numerator = numerator * rescale[..., None] + jnp.einsum(
            "tkgs,skd->tkgd", weights, value_block, preferred_element_type=jnp.float32
        )
        return ((new_max, running_sum, numerator), None)

    final_state, _ = lax.scan(advance, carried, (key_blocks, value_blocks, pos_blocks))
    return final_state


def general_device(queries, keys, values, block_order):
    block_total = block_order.shape[0]
    ctx_index = lax.axis_index("ctx")
    local_k, local_v = (
        lax.all_gather(keys, "tp", axis=0, tiled=True),
        lax.all_gather(values, "tp", axis=0, tiled=True),
    )
    first_row = lax.axis_index("tp") * queries.shape[0]
    token_rows = queries.shape[0]
    block_rows = local_k.shape[0]
    span_rows = block_rows // 2
    kv_local = local_k.shape[1] // HD
    group_size = queries.shape[1] // (HD * kv_local)
    queries_h = queries.reshape(token_rows, kv_local, group_size, HD)
    query_pos = block_positions(block_order, ctx_index, first_row, token_rows, span_rows)
    own_pair = jnp.stack(
        [local_k.reshape(block_rows, kv_local, HD), local_v.reshape(block_rows, kv_local, HD)]
    )
    state = (
        jnp.full((token_rows, kv_local, group_size), MASKED_SCORE, jnp.float32),
        jnp.zeros((token_rows, kv_local, group_size), jnp.float32),
        jnp.zeros((token_rows, kv_local, group_size, HD), jnp.float32),
    )
    own_pos = block_positions(block_order, ctx_index, 0, block_rows, span_rows)
    state = update(state, queries_h, query_pos, own_pair[0], own_pair[1], own_pos)
    moving = own_pair
    for step in range(1, PREV + 1):
        moving = passed_along(moving, "ctx", 1)
        source = (ctx_index - step) % block_total
        source_pos = block_positions(block_order, source, 0, block_rows, span_rows)
        state = update(state, queries_h, query_pos, moving[0], moving[1], source_pos)
    _, running_sum, numerator = state
    attended = (numerator / running_sum[..., None]).astype(jnp.bfloat16)
    attended = attended.reshape(token_rows, kv_local * group_size * HD)
    return attended


ROW_BLOCK = 6
PARTS = 2
VMEM_LIMIT = 32 * 2**20


def scored(left, right):
    return lax.dot_general(
        left, right, (((1,), (1,)), ((), ())), preferred_element_type=jnp.float32
    )


def weighed(left, right):
    return lax.dot_general(
        left, right, (((1,), (0,)), ((), ())), preferred_element_type=jnp.float32
    )


def attention_kernel(order_ref, queries_ref, *refs, tiles, counts, parts, kv_total, own, first, last):
    refs = list(refs)
    spans = [[refs.pop(0) for _ in range(count)] for count in counts]
    state_in = {} if first else {part: (refs.pop(0), refs.pop(0)) for part in parts}
    rows = queries_ref.shape[0]
    group = queries_ref.shape[1] // (HD * kv_total)
    kv_part = kv_total // PARTS
    scale = math.log2(math.e) / math.sqrt(HD)
    ctx_index, tp_index = lax.axis_index("ctx"), lax.axis_index("tp")
    block_total = order_ref.shape[0]

    def position(back, half):
        leading = order_ref[lax.rem(ctx_index + block_total - back, block_total)]
        return jnp.where(half == 0, leading, 2 * block_total - 1 - leading)

    def bias(tile):
        even_back, odd_back, flip = tile
        back = jnp.where(lax.rem(ctx_index, 2) == 0, even_back, odd_back)
        half = 1 - tp_index if flip else tp_index
        return jnp.where(position(back, half) < position(0, tp_index), 0.0, MASKED_SCORE)

    biases = [0.0 if own and t == 0 else bias(tile) for t, tile in enumerate(tiles)]

    def pairs_of(head):
        kv_head = head // group
        found = []
        for arrays in spans:
            whole = arrays[0].shape[1] == kv_total * HD
            ref = arrays[0] if whole else arrays[parts.index(kv_head // kv_part)]
            at = (kv_head if whole else kv_head % kv_part) * HD
            found.append((ref, slice(at, at + HD)))
        return found

    def key_rows(head):
        return jnp.concatenate([ref[:rows, at] for ref, at in pairs_of(head)], axis=0)

    def value_cols(head):
        cols = jnp.concatenate([ref[rows:, at].T for ref, at in pairs_of(head)], axis=1)
        return jnp.concatenate([cols, jnp.ones((16, cols.shape[1]), jnp.bfloat16)], axis=0)

    if own:
        key_ids = lax.broadcasted_iota(jnp.int32, (rows, rows), 0)
        row_ids = lax.broadcasted_iota(jnp.int32, (rows, rows), 1)
        causal = jnp.where(key_ids <= row_ids, 0.0, MASKED_SCORE).astype(jnp.float32)
        causal = jnp.concatenate([causal] * ROW_BLOCK, axis=1)

    def held(state, head):
        part, inside = divmod(head, kv_part * group)
        return *state[part], slice(inside * rows, (inside + ROW_BLOCK) * rows)

    def scores(head):
        block = jnp.concatenate(
            [queries_ref[:, (head + i) * HD : (head + i + 1) * HD] for i in range(ROW_BLOCK)], axis=0
        )
        product = scored(key_rows(head), block)
        pieces = [product[t * rows : (t + 1) * rows] for t in range(len(tiles))]
        if own:
            pieces[0] = pieces[0] + causal
        tops = [jnp.max(piece, axis=0, keepdims=True) + b for piece, b in zip(pieces, biases)]
        if not first:
            _, stat, at = held(state_in, head)
            tops.append(stat[0:1, at])
        return pieces, functools.reduce(jnp.maximum, tops)

    def finish(head, pieces, top):
        weights = jnp.concatenate(
            [
                jnp.exp2((piece - (top - b)) * scale).astype(jnp.bfloat16)
                for piece, b in zip(pieces, biases)
            ],
            axis=0,
        )
        product = weighed(value_cols(head), weights)
        total, numerator = product[HD : HD + 1], product[:HD]
        if not first:
            sums, stat, at = held(state_in, head)
            rescale = jnp.exp2((stat[0:1, at] - top) * scale)
            total = total + stat[1:2, at] * rescale
            numerator = numerator + sums[:, at] * rescale
        if last:
            out_ref, rounded, sems = refs
            result = (numerator / total).T.astype(jnp.bfloat16)
            for i in range(ROW_BLOCK):
                rounded[:, (head + i) * HD : (head + i + 1) * HD] = result[i * rows : (i + 1) * rows]
            columns = slice(head * HD, (head + ROW_BLOCK) * HD)
            copies.append(
                pltpu.make_async_copy(
                    rounded.at[:, columns], out_ref.at[:, columns], sems.at[len(copies)]
                )
            )
            copies[-1].start()
        else:
            state_out = {part: refs[2 * i : 2 * i + 2] for i, part in enumerate(parts)}
            sums, stat, at = held(state_out, head)
            sums[:, at] = numerator
            stat[0:1, at] = top
            stat[1:2, at] = total

    copies = []
    part_heads = kv_part * group
    heads = [
        part * part_heads + inside for part in parts for inside in range(0, part_heads, ROW_BLOCK)
    ]
    ahead = scores(heads[0])
    for index, head in enumerate(heads):
        now = ahead
        if index + 1 < len(heads):
            ahead = scores(heads[index + 1])
        finish(head, *now)
    for copy in copies:
        copy.wait()


def attend(block_order, queries, kv_total, spans, state, parts, own=False, last=False):
    rows, width = queries.shape
    arrays = [list(held) if len(held) == 1 else [held[part] for part in parts] for held, _ in spans]
    operands = [array for held in arrays for array in held]
    operands += [] if state is None else [array for held in state for array in held]
    here = pl.BlockSpec(memory_space=pltpu.VMEM)
    if last:
        out_specs = pl.BlockSpec(memory_space=pl.ANY)
        out_shape = jax.ShapeDtypeStruct(queries.shape, jnp.bfloat16)
        scratch_shapes = [
            pltpu.VMEM(queries.shape, jnp.bfloat16),
            pltpu.SemaphoreType.DMA((width // (ROW_BLOCK * HD),)),
        ]
    else:
        out_specs = (here,) * (2 * len(parts))
        out_shape = tuple(
            jax.ShapeDtypeStruct((depth, width // HD * rows // PARTS), jnp.float32)
            for _ in parts
            for depth in (HD, 8)
        )
        scratch_shapes = []
    score_count = width // HD * rows * rows * len(spans) * len(parts) // PARTS
    result = pl.pallas_call(
        functools.partial(
            attention_kernel,
            tiles=[place for _, place in spans], counts=[len(held) for held in arrays],
            parts=parts, kv_total=kv_total, own=own, first=state is None, last=last,
        ),
        in_specs=[pl.BlockSpec(memory_space=pltpu.SMEM)] + [here] * (1 + len(operands)),
        out_specs=out_specs,
        scratch_shapes=scratch_shapes,
        out_shape=out_shape,
        compiler_params=pltpu.CompilerParams(vmem_limit_bytes=VMEM_LIMIT),
        cost_estimate=pl.CostEstimate(
            flops=4 * score_count * HD,
            bytes_accessed=4 * rows * width * 2,
            transcendentals=score_count,
        ),
    )(block_order, queries, *operands)
    return result if last else [result[2 * i : 2 * i + 2] for i in range(len(parts))]


def span_device(queries, keys, values, block_order):
    block_total = block_order.shape[0]
    rows, kv_width = keys.shape
    kv_total = kv_width // HD

    def moved(value, target):
        pairs = []
        for block in range(block_total):
            for half in range(2):
                to_block, to_half = target(block, half)
                pairs.append((block * 2 + half, (to_block % block_total) * 2 + to_half))
        return lax.ppermute(value, ("ctx", "tp"), pairs)

    def moved_parts(values_of, target):
        return [moved(value, target) for value in values_of]

    def across(block, half):
        return block, 1 - half

    def two_on(block, half):
        return block + 2, half

    def to_next_pair(block, half):
        return block + (3 if block % 2 else 1), half

    def swapped(block, half):
        return block ^ 1, half

    def packed(columns):
        return jnp.stack([keys[:, columns], values[:, columns]]).reshape(2 * rows, -1)

    width = kv_width // PARTS
    own = [packed(slice(part * width, (part + 1) * width)) for part in range(PARTS)]
    same_2 = moved_parts(own, two_on)
    other_0 = moved_parts(own, across)
    same_a = moved_parts(own, to_next_pair)
    other_2 = moved_parts(same_2, across)
    same_b = moved_parts(same_2, swapped)
    other_a = moved_parts(other_0, to_next_pair)
    other_b = moved_parts(other_2, swapped)
    everything = tuple(range(PARTS))
    spans = [(own, (0, 0, False))]
    state = attend(block_order, queries, kv_total, spans, None, everything, own=True)
    spans = [(other_0, (0, 0, True)), (same_2, (2, 2, False)), (same_b, (1, 3, False))]
    for part in everything:
        (state[part],) = attend(
            block_order, queries, kv_total, spans, [state[part]], (part,)
        )
    spans = [
        (same_a, (3, 1, False)),
        (other_a, (3, 1, True)),
        (other_2, (2, 2, True)),
        (other_b, (1, 3, True)),
    ]
    return attend(block_order, queries, kv_total, spans, state, everything, last=True)


def solution(mesh):
    block_total, halves = mesh.shape["ctx"], mesh.shape["tp"]
    in_pairs = halves == 2 and block_total % 2 == 0 and block_total > PREV

    def per_device(queries, keys, values, block_order):
        if in_pairs:
            return span_device(queries, keys, values, block_order)
        return general_device(queries, keys, values, block_order)

    return jax.shard_map(
        per_device,
        mesh=mesh,
        in_specs=(P(("ctx", "tp"), None), P(("ctx", "tp"), None), P(("ctx", "tp"), None), P()),
        out_specs=P(("ctx", "tp"), None),
        check_vma=False,
    )
```

profile of v0, /device:TPU:0, one launch (start us, length us, event | category | flops | bytes accessed | tf_op | source)
XLA Modules:
  0.0 56.2 jit_solution(17945438336753837196)
XLA Ops:
  0.0 1.1 %slice_bitcast_fusion = (bf16[1,128,512]{2,1,0:T(8,128)(2,1)S(1)}, bf16[1,128,512]{2,1,0:T(8,128)(2,1)S(1)}, bf16[1,128,512]{2,1,0:T(8,128)(2,1)S(1)}, bf16[1,128,512]{2,1,0:T(8,128)(2,1)S(1)}) fusion(bf16[128,1024]{1,0:T(8,128)(2,1)} %param.6, bf16[128,1024]{1,0:T(8,128)(2,1)} %param.5), kind=kLoop, calls=%fused_computation.2 | loop fusion | bytes 1048576 | tf_op jit(solution)/shard_map/stack | solution.py:310
  1.2 3.0 %collective-permute-start.8 = (bf16[256,512]{1,0:T(8,128)(2,1)S(1)}, bf16[256,512]{1,0:T(8,128)(2,1)S(1)}, u32[]{:S(2)}, u32[]{:S(2)}) collective-permute-start(bf16[256,512]{1,0:T(8,128)(2,1)S(1)} %bitcast.14), channel_id=1, source_target_pairs={{0,4},{1,5},{2,6},{3,7},{4,8},{5,9},{6,10},{7,11},{8,12},{9,13},{1... | collective-permute-start | bytes 786440 | tf_op jit(solution)/shard_map/ppermute | solution.py:292
  4.2 1.6 %collective-permute-start.6 = (bf16[256,512]{1,0:T(8,128)(2,1)S(1)}, bf16[256,512]{1,0:T(8,128)(2,1)S(1)}, u32[]{:S(2)}, u32[]{:S(2)}) collective-permute-start(bf16[256,512]{1,0:T(8,128)(2,1)S(1)} %bitcast.10), channel_id=1, source_target_pairs={{0,4},{1,5},{2,6},{3,7},{4,8},{5,9},{6,10},{7,11},{8,12},{9,13},{1... | collective-permute-start | bytes 786440 | tf_op jit(solution)/shard_map/ppermute | solution.py:292
  5.8 1.5 %collective-permute-start.4 = (bf16[256,512]{1,0:T(8,128)(2,1)S(1)}, bf16[256,512]{1,0:T(8,128)(2,1)S(1)}, u32[]{:S(2)}, u32[]{:S(2)}) collective-permute-start(bf16[256,512]{1,0:T(8,128)(2,1)S(1)} %bitcast.15), channel_id=1, source_target_pairs={{0,1},{1,0},{2,3},{3,2},{4,5},{5,4},{6,7},{7,6},{8,9},{9,8},{10,11... | collective-permute-start | bytes 786440 | tf_op jit(solution)/shard_map/ppermute | solution.py:292
  7.3 0.5 collective-permute-start.2
  7.8 0.0 collective-permute-start.1
  7.8 6.5 %collective-permute-done.8.refs_1_ = bf16[256,512]{1,0:T(8,128)(2,1)S(1)} collective-permute-done((bf16[256,512]{1,0:T(8,128)(2,1)S(1)}, bf16[256,512]{1,0:T(8,128)(2,1)S(1)}, u32[]{:S(2)}, u32[]{:S(2)}) %collective-permute-start.8) | collective-permute-done | bytes 262176 | tf_op jit(solution)/shard_map/ppermute | solution.py:292
  14.4 5.6 %collective-permute-done.6.refs_1_ = bf16[256,512]{1,0:T(8,128)(2,1)S(1)} collective-permute-done((bf16[256,512]{1,0:T(8,128)(2,1)S(1)}, bf16[256,512]{1,0:T(8,128)(2,1)S(1)}, u32[]{:S(2)}, u32[]{:S(2)}) %collective-permute-start.6) | collective-permute-done | bytes 262176 | tf_op jit(solution)/shard_map/ppermute | solution.py:292
  20.0 0.0 collective-permute-start.12
  20.0 0.0 collective-permute-done.4.refs_0_
  20.0 1.7 %collective-permute-start.9 = (bf16[256,512]{1,0:T(8,128)(2,1)S(1)}, bf16[256,512]{1,0:T(8,128)(2,1)S(1)}, u32[]{:S(2)}, u32[]{:S(2)}) collective-permute-start(bf16[256,512]{1,0:T(8,128)(2,1)S(1)} %collective-permute-done.8.refs_1_), channel_id=1, source_target_pairs={{0,1},{1,0},{2,3},{3,2},{4,5},{5,4},{6,7},{7,6},{8,9},{9,8},{10,11... | collective-permute-start | bytes 786440 | tf_op jit(solution)/shard_map/ppermute | solution.py:292
  21.7 0.0 collective-permute-done.2.refs_0_
  21.7 0.3 collective-permute-start.7
  22.0 0.0 collective-permute-done.1.refs_1_
  22.0 0.0 collective-permute-start
  22.0 0.0 collective-permute-done.13.refs_2_
  22.0 0.1 collective-permute-start.5
  22.1 0.1 collective-permute-start.3
  22.2 7.0 %collective-permute-done.9.refs_5_ = bf16[256,512]{1,0:T(8,128)(2,1)S(1)} collective-permute-done((bf16[256,512]{1,0:T(8,128)(2,1)S(1)}, bf16[256,512]{1,0:T(8,128)(2,1)S(1)}, u32[]{:S(2)}, u32[]{:S(2)}) %collective-permute-start.9) | collective-permute-done | bytes 262176 | tf_op jit(solution)/shard_map/ppermute | solution.py:292
  29.2 0.0 collective-permute-start.11
  29.2 5.2 %collective-permute-done.7.refs_4_ = bf16[256,512]{1,0:T(8,128)(2,1)S(1)} collective-permute-done((bf16[256,512]{1,0:T(8,128)(2,1)S(1)}, bf16[256,512]{1,0:T(8,128)(2,1)S(1)}, u32[]{:S(2)}, u32[]{:S(2)}) %collective-permute-start.7) | collective-permute-done | bytes 262176 | tf_op jit(solution)/shard_map/ppermute | solution.py:292
  34.3 0.0 collective-permute-start.10
  34.3 1.9 %copy-done = bf16[128,12288]{1,0:T(8,128)(2,1)S(1)} copy-done((bf16[128,12288]{1,0:T(8,128)(2,1)S(1)}, bf16[128,12288]{1,0:T(8,128)(2,1)}, u32[]{:S(2)}) %copy-start) | copy-done | bytes 3145752
  36.2 0.7 %copy-done.1 = s32[16]{0:T(128)S(1)} copy-done((s32[16]{0:T(128)S(1)}, s32[16]{0:T(128)}, u32[]{:S(2)}) %copy-start.1) | copy-done | bytes 88
  36.9 3.0 %shard_map.46 = (f32[128,6144]{1,0:T(8,128)S(1)}, f32[8,6144]{1,0:T(8,128)S(1)}, f32[128,6144]{1,0:T(8,128)S(1)}, f32[8,6144]{1,0:T(8,128)S(1)}) custom-call(s32[16]{0:T(128)S(1)} %copy-done.1, bf16[128,12288]{1,0:T(8,128)(2,1)S(1)} %copy-done, bf16[256,512]{1,0:T(8,128)(2,1)S(1)} %bitcast.13, bf16[256,512]{1,0:T(8,128)(2,1)S(1)} %bitcast.17), custom_call_target="tpu_custom_call" | custom-call | flops 805306368 | bytes 12582912 | tf_op jit(solution)/shard_map/pallas_call | solution.py:261
  39.9 3.4 %shard_map.48 = (f32[128,6144]{1,0:T(8,128)S(1)}, f32[8,6144]{1,0:T(8,128)S(1)}) custom-call(s32[16]{0:T(128)S(1)} %copy-done.1, bf16[128,12288]{1,0:T(8,128)(2,1)S(1)} %copy-done, bf16[256,512]{1,0:T(8,128)(2,1)S(1)} %collective-permute-done.4.refs_0_, bf16[256,512]{1,0:T(8,128)(2,1)S(1)} %collective-permute-done.8.refs_1_, ...), custom_call_target="tpu_custom_call" | custom-call | flops 1207959552 | bytes 12582912 | tf_op jit(solution)/shard_map/pallas_call | solution.py:261
  43.3 3.4 %shard_map.47 = (f32[128,6144]{1,0:T(8,128)S(1)}, f32[8,6144]{1,0:T(8,128)S(1)}) custom-call(s32[16]{0:T(128)S(1)} %copy-done.1, bf16[128,12288]{1,0:T(8,128)(2,1)S(1)} %copy-done, bf16[256,512]{1,0:T(8,128)(2,1)S(1)} %collective-permute-done.2.refs_0_, bf16[256,512]{1,0:T(8,128)(2,1)S(1)} %collective-permute-done.6.refs_1_, ...), custom_call_target="tpu_custom_call" | custom-call | flops 1207959552 | bytes 12582912 | tf_op jit(solution)/shard_map/pallas_call | solution.py:261
  46.7 0.0 collective-permute-done.refs_0_
  46.7 0.0 collective-permute-done.5.refs_3_
  46.8 0.0 collective-permute-done.11.refs_7_
  46.8 0.0 collective-permute-done.10.refs_6_
  46.8 9.2 %shard_map.49 = bf16[128,12288]{1,0:T(8,128)(2,1)} custom-call(s32[16]{0:T(128)S(1)} %copy-done.1, bf16[128,12288]{1,0:T(8,128)(2,1)S(1)} %copy-done, bf16[256,512]{1,0:T(8,128)(2,1)S(1)} %collective-permute-done.refs_0_, bf16[256,512]{1,0:T(8,128)(2,1)S(1)} %collective-permute-done.1.refs_1_, bf16[256,512]{1,0:T(8,128)(2,1)S(1)} %collective-permute-done.3.refs_2_, ...), custom_call_target="tpu_custom_call" | custom-call | flops 3221225472 | bytes 12582912 | tf_op jit(solution)/shard_map/pallas_call | solution.py:261
  (7 shorter events, 0.1 us)
Async XLA Ops:
  1.2 13.2 %collective-permute-start.8 = (bf16[256,512]{1,0:T(8,128)(2,1)S(1)}, bf16[256,512]{1,0:T(8,128)(2,1)S(1)}, u32[]{:S(2)}, u32[]{:S(2)}) collective-permute-start(bf16[256,512]{1,0:T(8,128)(2,1)S(1)} %bitcast.14), channel_id=1, source_target_pairs={{0,4},{1,5},{2,6},{3,7},{4,8},{5,9},{6,10},{7,11},{8,12},{9,13},{1... | collective-permute-start | bytes 786440 | tf_op jit(solution)/shard_map/ppermute | solution.py:292
  4.2 15.8 %collective-permute-start.6 = (bf16[256,512]{1,0:T(8,128)(2,1)S(1)}, bf16[256,512]{1,0:T(8,128)(2,1)S(1)}, u32[]{:S(2)}, u32[]{:S(2)}) collective-permute-start(bf16[256,512]{1,0:T(8,128)(2,1)S(1)} %bitcast.10), channel_id=1, source_target_pairs={{0,4},{1,5},{2,6},{3,7},{4,8},{5,9},{6,10},{7,11},{8,12},{9,13},{1... | collective-permute-start | bytes 786440 | tf_op jit(solution)/shard_map/ppermute | solution.py:292
  5.8 14.2 %collective-permute-start.4 = (bf16[256,512]{1,0:T(8,128)(2,1)S(1)}, bf16[256,512]{1,0:T(8,128)(2,1)S(1)}, u32[]{:S(2)}, u32[]{:S(2)}) collective-permute-start(bf16[256,512]{1,0:T(8,128)(2,1)S(1)} %bitcast.15), channel_id=1, source_target_pairs={{0,1},{1,0},{2,3},{3,2},{4,5},{5,4},{6,7},{7,6},{8,9},{9,8},{10,11... | collective-permute-start | bytes 786440 | tf_op jit(solution)/shard_map/ppermute | solution.py:292
  7.3 14.4 %collective-permute-start.2 = (bf16[256,512]{1,0:T(8,128)(2,1)S(1)}, bf16[256,512]{1,0:T(8,128)(2,1)S(1)}, u32[]{:S(2)}, u32[]{:S(2)}) collective-permute-start(bf16[256,512]{1,0:T(8,128)(2,1)S(1)} %bitcast.11), channel_id=1, source_target_pairs={{0,1},{1,0},{2,3},{3,2},{4,5},{5,4},{6,7},{7,6},{8,9},{9,8},{10,11... | collective-permute-start | bytes 786440 | tf_op jit(solution)/shard_map/ppermute | solution.py:292
  7.8 14.2 %collective-permute-start.1 = (bf16[256,512]{1,0:T(8,128)(2,1)S(1)}, bf16[256,512]{1,0:T(8,128)(2,1)S(1)}, u32[]{:S(2)}, u32[]{:S(2)}) collective-permute-start(bf16[256,512]{1,0:T(8,128)(2,1)S(1)} %bitcast.16), channel_id=1, source_target_pairs={{0,2},{1,3},{2,8},{3,9},{4,6},{5,7},{6,12},{7,13},{8,10},{9,11},{1... | collective-permute-start | bytes 786440 | tf_op jit(solution)/shard_map/ppermute | solution.py:292
  14.4 7.7 %collective-permute-start.13 = (bf16[256,512]{1,0:T(8,128)(2,1)S(1)}, bf16[256,512]{1,0:T(8,128)(2,1)S(1)}, u32[]{:S(2)}, u32[]{:S(2)}) collective-permute-start(bf16[256,512]{1,0:T(8,128)(2,1)S(1)} %collective-permute-done.8.refs_1_), channel_id=1, source_target_pairs={{0,2},{1,3},{2,0},{3,1},{4,6},{5,7},{6,4},{7,5},{8,10},{9,11},{10,... | collective-permute-start | bytes 786440 | tf_op jit(solution)/shard_map/ppermute | solution.py:292
  20.0 2.1 %collective-permute-start.12 = (bf16[256,512]{1,0:T(8,128)(2,1)S(1)}, bf16[256,512]{1,0:T(8,128)(2,1)S(1)}, u32[]{:S(2)}, u32[]{:S(2)}) collective-permute-start(bf16[256,512]{1,0:T(8,128)(2,1)S(1)} %collective-permute-done.6.refs_1_), channel_id=1, source_target_pairs={{0,2},{1,3},{2,0},{3,1},{4,6},{5,7},{6,4},{7,5},{8,10},{9,11},{10,... | collective-permute-start | bytes 786440 | tf_op jit(solution)/shard_map/ppermute | solution.py:292
  20.0 9.2 %collective-permute-start.9 = (bf16[256,512]{1,0:T(8,128)(2,1)S(1)}, bf16[256,512]{1,0:T(8,128)(2,1)S(1)}, u32[]{:S(2)}, u32[]{:S(2)}) collective-permute-start(bf16[256,512]{1,0:T(8,128)(2,1)S(1)} %collective-permute-done.8.refs_1_), channel_id=1, source_target_pairs={{0,1},{1,0},{2,3},{3,2},{4,5},{5,4},{6,7},{7,6},{8,9},{9,8},{10,11... | collective-permute-start | bytes 786440 | tf_op jit(solution)/shard_map/ppermute | solution.py:292
  21.7 12.6 %collective-permute-start.7 = (bf16[256,512]{1,0:T(8,128)(2,1)S(1)}, bf16[256,512]{1,0:T(8,128)(2,1)S(1)}, u32[]{:S(2)}, u32[]{:S(2)}) collective-permute-start(bf16[256,512]{1,0:T(8,128)(2,1)S(1)} %collective-permute-done.6.refs_1_), channel_id=1, source_target_pairs={{0,1},{1,0},{2,3},{3,2},{4,5},{5,4},{6,7},{7,6},{8,9},{9,8},{10,11... | collective-permute-start | bytes 786440 | tf_op jit(solution)/shard_map/ppermute | solution.py:292
  22.0 24.7 %collective-permute-start = (bf16[256,512]{1,0:T(8,128)(2,1)S(1)}, bf16[256,512]{1,0:T(8,128)(2,1)S(1)}, u32[]{:S(2)}, u32[]{:S(2)}) collective-permute-start(bf16[256,512]{1,0:T(8,128)(2,1)S(1)} %bitcast.12), channel_id=1, source_target_pairs={{0,2},{1,3},{2,8},{3,9},{4,6},{5,7},{6,12},{7,13},{8,10},{9,11},{1... | collective-permute-start | bytes 786440 | tf_op jit(solution)/shard_map/ppermute | solution.py:292
  22.0 24.7 %collective-permute-start.5 = (bf16[256,512]{1,0:T(8,128)(2,1)S(1)}, bf16[256,512]{1,0:T(8,128)(2,1)S(1)}, u32[]{:S(2)}, u32[]{:S(2)}) collective-permute-start(bf16[256,512]{1,0:T(8,128)(2,1)S(1)} %collective-permute-done.4.refs_0_), channel_id=1, source_target_pairs={{0,2},{1,3},{2,8},{3,9},{4,6},{5,7},{6,12},{7,13},{8,10},{9,11},{1... | collective-permute-start | bytes 786440 | tf_op jit(solution)/shard_map/ppermute | solution.py:292
  22.1 24.6 %collective-permute-start.3 = (bf16[256,512]{1,0:T(8,128)(2,1)S(1)}, bf16[256,512]{1,0:T(8,128)(2,1)S(1)}, u32[]{:S(2)}, u32[]{:S(2)}) collective-permute-start(bf16[256,512]{1,0:T(8,128)(2,1)S(1)} %collective-permute-done.2.refs_0_), channel_id=1, source_target_pairs={{0,2},{1,3},{2,8},{3,9},{4,6},{5,7},{6,12},{7,13},{8,10},{9,11},{1... | collective-permute-start | bytes 786440 | tf_op jit(solution)/shard_map/ppermute | solution.py:292
  29.2 17.6 %collective-permute-start.11 = (bf16[256,512]{1,0:T(8,128)(2,1)S(1)}, bf16[256,512]{1,0:T(8,128)(2,1)S(1)}, u32[]{:S(2)}, u32[]{:S(2)}) collective-permute-start(bf16[256,512]{1,0:T(8,128)(2,1)S(1)} %collective-permute-done.9.refs_5_), channel_id=1, source_target_pairs={{0,2},{1,3},{2,0},{3,1},{4,6},{5,7},{6,4},{7,5},{8,10},{9,11},{10,... | collective-permute-start | bytes 786440 | tf_op jit(solution)/shard_map/ppermute | solution.py:292
  34.3 12.4 %collective-permute-start.10 = (bf16[256,512]{1,0:T(8,128)(2,1)S(1)}, bf16[256,512]{1,0:T(8,128)(2,1)S(1)}, u32[]{:S(2)}, u32[]{:S(2)}) collective-permute-start(bf16[256,512]{1,0:T(8,128)(2,1)S(1)} %collective-permute-done.7.refs_4_), channel_id=1, source_target_pairs={{0,2},{1,3},{2,0},{3,1},{4,6},{5,7},{6,4},{7,5},{8,10},{9,11},{10,... | collective-permute-start | bytes 786440 | tf_op jit(solution)/shard_map/ppermute | solution.py:292
  34.3 1.9 %copy-start = (bf16[128,12288]{1,0:T(8,128)(2,1)S(1)}, bf16[128,12288]{1,0:T(8,128)(2,1)}, u32[]{:S(2)}) copy-start(bf16[128,12288]{1,0:T(8,128)(2,1)} %queries_ref.7) | copy-start | bytes 9437188
  36.2 0.7 %copy-start.1 = (s32[16]{0:T(128)S(1)}, s32[16]{0:T(128)}, u32[]{:S(2)}) copy-start(s32[16]{0:T(128)} %order_ref.7) | copy-start | bytes 196
where the time goes:
time: 56.4 us; the launch traced here: 56.2 us
  waiting for transfers between devices  24.3 us (43%)
  Pallas kernels  19 us (34%)
  starting transfers between devices  8.84 us (16%)
  local copies, waits for them, and re-layouts  3.67 us (7%)
    ppermute x14, waiting for transfers between devices, moved(): return lax.ppermute(value, ('ctx', 'tp'), pairs)  24.3 us
    pallas_call x4, Pallas kernels, attend(): pl.pallas_call(functools.partial(attention_kernel, tiles=[place for _, pl...  19 us
    ppermute x14, starting transfers between devices, moved(): return lax.ppermute(value, ('ctx', 'tp'), pairs)  8.84 us
    unnamed x4, local copies, waits for them, and re-layouts  2.54 us
  transfers between devices with their start and end apart: 14, of which 4 were waited for; matrix products, arithmetic and copies ran while one was open for 0% of the time, Pallas kernels for 17%

commit v1 on v0

--- a/solution.py
+++ b/solution.py
@@ -108,6 +108,7 @@
 
 ROW_BLOCK = 6
 PARTS = 2
+OWN_LIMIT = 44 * 2**20
 VMEM_LIMIT = 32 * 2**20
 
 
@@ -123,8 +124,10 @@
     )
 
 
-def attention_kernel(order_ref, queries_ref, *refs, tiles, counts, parts, kv_total, own, first, last):
+def attention_kernel(*refs, tiles, counts, parts, kv_total, own, first, last):
     refs = list(refs)
+    order_ref = None if own else refs.pop(0)
+    queries_ref = refs.pop(0)
     spans = [[refs.pop(0) for _ in range(count)] for count in counts]
     state_in = {} if first else {part: (refs.pop(0), refs.pop(0)) for part in parts}
     rows = queries_ref.shape[0]
@@ -132,9 +135,9 @@
     kv_part = kv_total // PARTS
     scale = math.log2(math.e) / math.sqrt(HD)
     ctx_index, tp_index = lax.axis_index("ctx"), lax.axis_index("tp")
-    block_total = order_ref.shape[0]
 
     def position(back, half):
+        block_total = order_ref.shape[0]
         leading = order_ref[lax.rem(ctx_index + block_total - back, block_total)]
         return jnp.where(half == 0, leading, 2 * block_total - 1 - leading)
 
@@ -163,7 +166,15 @@
         cols = jnp.concatenate([ref[rows:, at].T for ref, at in pairs_of(head)], axis=1)
         return jnp.concatenate([cols, jnp.ones((16, cols.shape[1]), jnp.bfloat16)], axis=0)
 
+    arrivals = {}
     if own:
+        queries_far, (queries_ref, arrival_sems) = queries_ref, refs[-2:]
+        for kv_head in range(kv_total):
+            columns = slice(kv_head * group * HD, (kv_head + 1) * group * HD)
+            arrivals[kv_head] = pltpu.make_async_copy(
+                queries_far.at[:, columns], queries_ref.at[:, columns], arrival_sems.at[kv_head]
+            )
+            arrivals[kv_head].start()
         key_ids = lax.broadcasted_iota(jnp.int32, (rows, rows), 0)
         row_ids = lax.broadcasted_iota(jnp.int32, (rows, rows), 1)
         causal = jnp.where(key_ids <= row_ids, 0.0, MASKED_SCORE).astype(jnp.float32)
@@ -174,6 +185,8 @@
         return *state[part], slice(inside * rows, (inside + ROW_BLOCK) * rows)
 
     def scores(head):
+        if head // group in arrivals:
+            arrivals.pop(head // group).wait()
         block = jnp.concatenate(
             [queries_ref[:, (head + i) * HD : (head + i + 1) * HD] for i in range(ROW_BLOCK)], axis=0
         )
@@ -257,6 +270,17 @@
             for depth in (HD, 8)
         )
         scratch_shapes = []
+        if own:
+            out_specs += (here,)
+            out_shape += (jax.ShapeDtypeStruct(queries.shape, jnp.bfloat16),)
+            scratch_shapes = [pltpu.SemaphoreType.DMA((kv_total,))]
+    in_specs = [here] * (1 + len(operands))
+    operands.insert(0, queries)
+    if own:
+        in_specs[0] = pl.BlockSpec(memory_space=pltpu.HBM)
+    else:
+        in_specs.insert(0, pl.BlockSpec(memory_space=pltpu.SMEM))
+        operands.insert(0, block_order)
     score_count = width // HD * rows * rows * len(spans) * len(parts) // PARTS
     result = pl.pallas_call(
         functools.partial(
@@ -264,18 +288,21 @@
             tiles=[place for _, place in spans], counts=[len(held) for held in arrays],
             parts=parts, kv_total=kv_total, own=own, first=state is None, last=last,
         ),
-        in_specs=[pl.BlockSpec(memory_space=pltpu.SMEM)] + [here] * (1 + len(operands)),
+        in_specs=in_specs,
         out_specs=out_specs,
         scratch_shapes=scratch_shapes,
         out_shape=out_shape,
-        compiler_params=pltpu.CompilerParams(vmem_limit_bytes=VMEM_LIMIT),
+        compiler_params=pltpu.CompilerParams(vmem_limit_bytes=OWN_LIMIT if own else VMEM_LIMIT),
         cost_estimate=pl.CostEstimate(
             flops=4 * score_count * HD,
             bytes_accessed=4 * rows * width * 2,
             transcendentals=score_count,
         ),
-    )(block_order, queries, *operands)
-    return result if last else [result[2 * i : 2 * i + 2] for i in range(len(parts))]
+    )(*operands)
+    if last:
+        return result
+    states = [result[2 * i : 2 * i + 2] for i in range(len(parts))]
+    return (states, result[-1]) if own else states
 
 
 def span_device(queries, keys, values, block_order):
@@ -320,12 +347,10 @@
     other_b = moved_parts(other_2, swapped)
     everything = tuple(range(PARTS))
     spans = [(own, (0, 0, False))]
-    state = attend(block_order, queries, kv_total, spans, None, everything, own=True)
+    state, queries = attend(block_order, queries, kv_total, spans, None, everything, own=True)
     spans = [(other_0, (0, 0, True)), (same_2, (2, 2, False)), (same_b, (1, 3, False))]
     for part in everything:
-        (state[part],) = attend(
-            block_order, queries, kv_total, spans, [state[part]], (part,)
-        )
+        (state[part],) = attend(block_order, queries, kv_total, spans, [state[part]], (part,))
     spans = [
         (same_a, (3, 1, False)),
         (other_a, (3, 1, True)),

time: 56.4 us -> 54.6 us (0.968)
  local copies, waits for them, and re-layouts: 3.67 us -> 1.14 us
  Pallas kernels: 19 us -> 19.8 us
    unnamed x4 -> x2, local copies, waits for them, and re-layouts: 2.54 us -> 0.01 us
    pallas_call x4, Pallas kernels: 19 us -> 19.8 us  [attend(): pl.pallas_call(functools.partial(attention_kernel, tiles=[place for _, pl...]
  transfers between devices with their start and end apart: 14 -> 14, of which waited for: 4 -> 4; matrix products, arithmetic and copies ran while one was open for 0% -> 0% of each run, Pallas kernels for 17% -> 20%
where the time goes in v1:
time: 54.6 us; the launch traced here: 54.4 us
  waiting for transfers between devices  24.3 us (45%)
  Pallas kernels  19.8 us (36%)
  starting transfers between devices  8.84 us (16%)
  local copies, waits for them, and re-layouts  1.14 us (2%)
    ppermute x14, waiting for transfers between devices, moved(): return lax.ppermute(value, ('ctx', 'tp'), pairs)  24.3 us
    pallas_call x4, Pallas kernels, attend(): pl.pallas_call(functools.partial(attention_kernel, tiles=[place for _, pl...  19.8 us
    ppermute x14, starting transfers between devices, moved(): return lax.ppermute(value, ('ctx', 'tp'), pairs)  8.84 us
    another operation x1, local copies, waits for them, and re-layouts, packed(): jnp.stack([keys[:, columns], values[:, columns]]).reshape(2 * rows, -1)  1.14 us
  transfers between devices with their start and end apart: 14, of which 4 were waited for; matrix products, arithmetic and copies ran while one was open for 0% of the time, Pallas kernels for 20%

profile of v1, /device:TPU:0, one launch (start us, length us, event | category | flops | bytes accessed | tf_op | source)
XLA Modules:
  0.0 54.4 jit_solution(228033692475363018)
XLA Ops:
  0.0 1.1 %slice_bitcast_fusion = (bf16[1,128,512]{2,1,0:T(8,128)(2,1)S(1)}, bf16[1,128,512]{2,1,0:T(8,128)(2,1)S(1)}, bf16[1,128,512]{2,1,0:T(8,128)(2,1)S(1)}, bf16[1,128,512]{2,1,0:T(8,128)(2,1)S(1)}) fusion(bf16[128,1024]{1,0:T(8,128)(2,1)} %param.6, bf16[128,1024]{1,0:T(8,128)(2,1)} %param.5), kind=kLoop, calls=%fused_computation.2 | loop fusion | bytes 1048576 | tf_op jit(solution)/shard_map/stack | solution.py:337
  1.2 3.0 %collective-permute-start.8 = (bf16[256,512]{1,0:T(8,128)(2,1)S(1)}, bf16[256,512]{1,0:T(8,128)(2,1)S(1)}, u32[]{:S(2)}, u32[]{:S(2)}) collective-permute-start(bf16[256,512]{1,0:T(8,128)(2,1)S(1)} %bitcast.14), channel_id=1, source_target_pairs={{0,4},{1,5},{2,6},{3,7},{4,8},{5,9},{6,10},{7,11},{8,12},{9,13},{1... | collective-permute-start | bytes 786440 | tf_op jit(solution)/shard_map/ppermute | solution.py:319
  4.2 1.6 %collective-permute-start.6 = (bf16[256,512]{1,0:T(8,128)(2,1)S(1)}, bf16[256,512]{1,0:T(8,128)(2,1)S(1)}, u32[]{:S(2)}, u32[]{:S(2)}) collective-permute-start(bf16[256,512]{1,0:T(8,128)(2,1)S(1)} %bitcast.10), channel_id=1, source_target_pairs={{0,4},{1,5},{2,6},{3,7},{4,8},{5,9},{6,10},{7,11},{8,12},{9,13},{1... | collective-permute-start | bytes 786440 | tf_op jit(solution)/shard_map/ppermute | solution.py:319
  5.8 1.5 %collective-permute-start.4 = (bf16[256,512]{1,0:T(8,128)(2,1)S(1)}, bf16[256,512]{1,0:T(8,128)(2,1)S(1)}, u32[]{:S(2)}, u32[]{:S(2)}) collective-permute-start(bf16[256,512]{1,0:T(8,128)(2,1)S(1)} %bitcast.15), channel_id=1, source_target_pairs={{0,1},{1,0},{2,3},{3,2},{4,5},{5,4},{6,7},{7,6},{8,9},{9,8},{10,11... | collective-permute-start | bytes 786440 | tf_op jit(solution)/shard_map/ppermute | solution.py:319
  7.4 0.5 collective-permute-start.2
  7.9 0.0 collective-permute-start.1
  7.9 6.5 %collective-permute-done.8.refs_3_ = bf16[256,512]{1,0:T(8,128)(2,1)S(1)} collective-permute-done((bf16[256,512]{1,0:T(8,128)(2,1)S(1)}, bf16[256,512]{1,0:T(8,128)(2,1)S(1)}, u32[]{:S(2)}, u32[]{:S(2)}) %collective-permute-start.8) | collective-permute-done | bytes 262176 | tf_op jit(solution)/shard_map/ppermute | solution.py:319
  14.4 0.0 collective-permute-start.13
  14.4 5.6 %collective-permute-done.6.refs_3_ = bf16[256,512]{1,0:T(8,128)(2,1)S(1)} collective-permute-done((bf16[256,512]{1,0:T(8,128)(2,1)S(1)}, bf16[256,512]{1,0:T(8,128)(2,1)S(1)}, u32[]{:S(2)}, u32[]{:S(2)}) %collective-permute-start.6) | collective-permute-done | bytes 262176 | tf_op jit(solution)/shard_map/ppermute | solution.py:319
  20.0 0.0 collective-permute-start.12
  20.0 0.0 collective-permute-done.4.refs_2_
  20.0 1.7 %collective-permute-start.9 = (bf16[256,512]{1,0:T(8,128)(2,1)S(1)}, bf16[256,512]{1,0:T(8,128)(2,1)S(1)}, u32[]{:S(2)}, u32[]{:S(2)}) collective-permute-start(bf16[256,512]{1,0:T(8,128)(2,1)S(1)} %collective-permute-done.8.refs_3_), channel_id=1, source_target_pairs={{0,1},{1,0},{2,3},{3,2},{4,5},{5,4},{6,7},{7,6},{8,9},{9,8},{10,11... | collective-permute-start | bytes 786440 | tf_op jit(solution)/shard_map/ppermute | solution.py:319
  21.7 0.0 collective-permute-done.2.refs_2_
  21.7 0.3 collective-permute-start.7
  22.1 0.0 collective-permute-done.1.refs_3_
  22.1 0.0 collective-permute-start
  22.1 0.0 collective-permute-done.13.refs_4_
  22.1 0.1 collective-permute-start.5
  22.2 0.0 collective-permute-done.12.refs_4_
  22.2 0.1 collective-permute-start.3
  22.2 7.0 %collective-permute-done.9.refs_7_ = bf16[256,512]{1,0:T(8,128)(2,1)S(1)} collective-permute-done((bf16[256,512]{1,0:T(8,128)(2,1)S(1)}, bf16[256,512]{1,0:T(8,128)(2,1)S(1)}, u32[]{:S(2)}, u32[]{:S(2)}) %collective-permute-start.9) | collective-permute-done | bytes 262176 | tf_op jit(solution)/shard_map/ppermute | solution.py:319
  29.2 0.0 collective-permute-start.11
  29.2 5.2 %collective-permute-done.7.refs_6_ = bf16[256,512]{1,0:T(8,128)(2,1)S(1)} collective-permute-done((bf16[256,512]{1,0:T(8,128)(2,1)S(1)}, bf16[256,512]{1,0:T(8,128)(2,1)S(1)}, u32[]{:S(2)}, u32[]{:S(2)}) %collective-permute-start.7) | collective-permute-done | bytes 262176 | tf_op jit(solution)/shard_map/ppermute | solution.py:319
  34.4 0.0 collective-permute-start.10
  34.4 4.7 %shard_map.46 = (f32[128,6144]{1,0:T(8,128)S(1)}, f32[8,6144]{1,0:T(8,128)S(1)}, f32[128,6144]{1,0:T(8,128)S(1)}, f32[8,6144]{1,0:T(8,128)S(1)}, bf16[128,12288]{1,0:T(8,128)(2,1)S(1)}) custom-call(bf16[128,12288]{1,0:T(8,128)(2,1)} %refs_0_.4, bf16[256,512]{1,0:T(8,128)(2,1)S(1)} %bitcast.13, bf16[256,512]{1,0:T(8,128)(2,1)S(1)} %bitcast.17), custom_call_target="tpu_custom_call" | custom-call | flops 805306368 | bytes 12582912 | tf_op jit(solution)/shard_map/pallas_call | solution.py:285
  39.1 3.2 %shard_map.48 = (f32[128,6144]{1,0:T(8,128)S(1)}, f32[8,6144]{1,0:T(8,128)S(1)}) custom-call(s32[16]{0:T(128)S(1)} %copy-done, bf16[128,12288]{1,0:T(8,128)(2,1)S(1)} %get-tuple-element.14.refs_1_, bf16[256,512]{1,0:T(8,128)(2,1)S(1)} %collective-permute-done.4.refs_2_, bf16[256,512]{1,0:T(8,128)(2,1)S(1)} %collective-permute-done.8.refs_3_, ...), custom_call_target="tpu_custom_call" | custom-call | flops 1207959552 | bytes 12582912 | tf_op jit(solution)/shard_map/pallas_call | solution.py:285
  42.3 3.2 %shard_map.47 = (f32[128,6144]{1,0:T(8,128)S(1)}, f32[8,6144]{1,0:T(8,128)S(1)}) custom-call(s32[16]{0:T(128)S(1)} %copy-done, bf16[128,12288]{1,0:T(8,128)(2,1)S(1)} %get-tuple-element.14.refs_1_, bf16[256,512]{1,0:T(8,128)(2,1)S(1)} %collective-permute-done.2.refs_2_, bf16[256,512]{1,0:T(8,128)(2,1)S(1)} %collective-permute-done.6.refs_3_, ...), custom_call_target="tpu_custom_call" | custom-call | flops 1207959552 | bytes 12582912 | tf_op jit(solution)/shard_map/pallas_call | solution.py:285
  45.5 0.0 collective-permute-done.refs_2_
  45.5 0.0 collective-permute-done.5.refs_5_
  45.5 0.0 collective-permute-done.3.refs_4_
  45.6 0.0 collective-permute-done.11.refs_9_
  45.6 8.7 %shard_map.49 = bf16[128,12288]{1,0:T(8,128)(2,1)} custom-call(s32[16]{0:T(128)S(1)} %copy-done, bf16[128,12288]{1,0:T(8,128)(2,1)S(1)} %get-tuple-element.14.refs_1_, bf16[256,512]{1,0:T(8,128)(2,1)S(1)} %collective-permute-done.refs_2_, bf16[256,512]{1,0:T(8,128)(2,1)S(1)} %collective-permute-done.1.refs_3_, ...), custom_call_target="tpu_custom_call" | custom-call | flops 3221225472 | bytes 12582912 | tf_op jit(solution)/shard_map/pallas_call | solution.py:285
  (5 shorter events, 0.1 us)
Async XLA Ops:
  0.0 39.1 %copy-start = (s32[16]{0:T(128)S(1)}, s32[16]{0:T(128)}, u32[]{:S(2)}) copy-start(s32[16]{0:T(128)} %refs_0_.7) | copy-start | bytes 196
  1.2 13.2 %collective-permute-start.8 = (bf16[256,512]{1,0:T(8,128)(2,1)S(1)}, bf16[256,512]{1,0:T(8,128)(2,1)S(1)}, u32[]{:S(2)}, u32[]{:S(2)}) collective-permute-start(bf16[256,512]{1,0:T(8,128)(2,1)S(1)} %bitcast.14), channel_id=1, source_target_pairs={{0,4},{1,5},{2,6},{3,7},{4,8},{5,9},{6,10},{7,11},{8,12},{9,13},{1... | collective-permute-start | bytes 786440 | tf_op jit(solution)/shard_map/ppermute | solution.py:319
  4.2 15.8 %collective-permute-start.6 = (bf16[256,512]{1,0:T(8,128)(2,1)S(1)}, bf16[256,512]{1,0:T(8,128)(2,1)S(1)}, u32[]{:S(2)}, u32[]{:S(2)}) collective-permute-start(bf16[256,512]{1,0:T(8,128)(2,1)S(1)} %bitcast.10), channel_id=1, source_target_pairs={{0,4},{1,5},{2,6},{3,7},{4,8},{5,9},{6,10},{7,11},{8,12},{9,13},{1... | collective-permute-start | bytes 786440 | tf_op jit(solution)/shard_map/ppermute | solution.py:319
  5.8 14.2 %collective-permute-start.4 = (bf16[256,512]{1,0:T(8,128)(2,1)S(1)}, bf16[256,512]{1,0:T(8,128)(2,1)S(1)}, u32[]{:S(2)}, u32[]{:S(2)}) collective-permute-start(bf16[256,512]{1,0:T(8,128)(2,1)S(1)} %bitcast.15), channel_id=1, source_target_pairs={{0,1},{1,0},{2,3},{3,2},{4,5},{5,4},{6,7},{7,6},{8,9},{9,8},{10,11... | collective-permute-start | bytes 786440 | tf_op jit(solution)/shard_map/ppermute | solution.py:319
  7.4 14.4 %collective-permute-start.2 = (bf16[256,512]{1,0:T(8,128)(2,1)S(1)}, bf16[256,512]{1,0:T(8,128)(2,1)S(1)}, u32[]{:S(2)}, u32[]{:S(2)}) collective-permute-start(bf16[256,512]{1,0:T(8,128)(2,1)S(1)} %bitcast.11), channel_id=1, source_target_pairs={{0,1},{1,0},{2,3},{3,2},{4,5},{5,4},{6,7},{7,6},{8,9},{9,8},{10,11... | collective-permute-start | bytes 786440 | tf_op jit(solution)/shard_map/ppermute | solution.py:319
  7.9 14.2 %collective-permute-start.1 = (bf16[256,512]{1,0:T(8,128)(2,1)S(1)}, bf16[256,512]{1,0:T(8,128)(2,1)S(1)}, u32[]{:S(2)}, u32[]{:S(2)}) collective-permute-start(bf16[256,512]{1,0:T(8,128)(2,1)S(1)} %bitcast.16), channel_id=1, source_target_pairs={{0,2},{1,3},{2,8},{3,9},{4,6},{5,7},{6,12},{7,13},{8,10},{9,11},{1... | collective-permute-start | bytes 786440 | tf_op jit(solution)/shard_map/ppermute | solution.py:319
  14.4 7.7 %collective-permute-start.13 = (bf16[256,512]{1,0:T(8,128)(2,1)S(1)}, bf16[256,512]{1,0:T(8,128)(2,1)S(1)}, u32[]{:S(2)}, u32[]{:S(2)}) collective-permute-start(bf16[256,512]{1,0:T(8,128)(2,1)S(1)} %collective-permute-done.8.refs_3_), channel_id=1, source_target_pairs={{0,2},{1,3},{2,0},{3,1},{4,6},{5,7},{6,4},{7,5},{8,10},{9,11},{10,... | collective-permute-start | bytes 786440 | tf_op jit(solution)/shard_map/ppermute | solution.py:319
  20.0 2.1 %collective-permute-start.12 = (bf16[256,512]{1,0:T(8,128)(2,1)S(1)}, bf16[256,512]{1,0:T(8,128)(2,1)S(1)}, u32[]{:S(2)}, u32[]{:S(2)}) collective-permute-start(bf16[256,512]{1,0:T(8,128)(2,1)S(1)} %collective-permute-done.6.refs_3_), channel_id=1, source_target_pairs={{0,2},{1,3},{2,0},{3,1},{4,6},{5,7},{6,4},{7,5},{8,10},{9,11},{10,... | collective-permute-start | bytes 786440 | tf_op jit(solution)/shard_map/ppermute | solution.py:319
  20.0 9.2 %collective-permute-start.9 = (bf16[256,512]{1,0:T(8,128)(2,1)S(1)}, bf16[256,512]{1,0:T(8,128)(2,1)S(1)}, u32[]{:S(2)}, u32[]{:S(2)}) collective-permute-start(bf16[256,512]{1,0:T(8,128)(2,1)S(1)} %collective-permute-done.8.refs_3_), channel_id=1, source_target_pairs={{0,1},{1,0},{2,3},{3,2},{4,5},{5,4},{6,7},{7,6},{8,9},{9,8},{10,11... | collective-permute-start | bytes 786440 | tf_op jit(solution)/shard_map/ppermute | solution.py:319
  21.7 12.6 %collective-permute-start.7 = (bf16[256,512]{1,0:T(8,128)(2,1)S(1)}, bf16[256,512]{1,0:T(8,128)(2,1)S(1)}, u32[]{:S(2)}, u32[]{:S(2)}) collective-permute-start(bf16[256,512]{1,0:T(8,128)(2,1)S(1)} %collective-permute-done.6.refs_3_), channel_id=1, source_target_pairs={{0,1},{1,0},{2,3},{3,2},{4,5},{5,4},{6,7},{7,6},{8,9},{9,8},{10,11... | collective-permute-start | bytes 786440 | tf_op jit(solution)/shard_map/ppermute | solution.py:319
  22.1 23.5 %collective-permute-start = (bf16[256,512]{1,0:T(8,128)(2,1)S(1)}, bf16[256,512]{1,0:T(8,128)(2,1)S(1)}, u32[]{:S(2)}, u32[]{:S(2)}) collective-permute-start(bf16[256,512]{1,0:T(8,128)(2,1)S(1)} %bitcast.12), channel_id=1, source_target_pairs={{0,2},{1,3},{2,8},{3,9},{4,6},{5,7},{6,12},{7,13},{8,10},{9,11},{1... | collective-permute-start | bytes 786440 | tf_op jit(solution)/shard_map/ppermute | solution.py:319
  22.1 23.5 %collective-permute-start.5 = (bf16[256,512]{1,0:T(8,128)(2,1)S(1)}, bf16[256,512]{1,0:T(8,128)(2,1)S(1)}, u32[]{:S(2)}, u32[]{:S(2)}) collective-permute-start(bf16[256,512]{1,0:T(8,128)(2,1)S(1)} %collective-permute-done.4.refs_2_), channel_id=1, source_target_pairs={{0,2},{1,3},{2,8},{3,9},{4,6},{5,7},{6,12},{7,13},{8,10},{9,11},{1... | collective-permute-start | bytes 786440 | tf_op jit(solution)/shard_map/ppermute | solution.py:319
  22.2 23.4 %collective-permute-start.3 = (bf16[256,512]{1,0:T(8,128)(2,1)S(1)}, bf16[256,512]{1,0:T(8,128)(2,1)S(1)}, u32[]{:S(2)}, u32[]{:S(2)}) collective-permute-start(bf16[256,512]{1,0:T(8,128)(2,1)S(1)} %collective-permute-done.2.refs_2_), channel_id=1, source_target_pairs={{0,2},{1,3},{2,8},{3,9},{4,6},{5,7},{6,12},{7,13},{8,10},{9,11},{1... | collective-permute-start | bytes 786440 | tf_op jit(solution)/shard_map/ppermute | solution.py:319
  29.2 16.4 %collective-permute-start.11 = (bf16[256,512]{1,0:T(8,128)(2,1)S(1)}, bf16[256,512]{1,0:T(8,128)(2,1)S(1)}, u32[]{:S(2)}, u32[]{:S(2)}) collective-permute-start(bf16[256,512]{1,0:T(8,128)(2,1)S(1)} %collective-permute-done.9.refs_7_), channel_id=1, source_target_pairs={{0,2},{1,3},{2,0},{3,1},{4,6},{5,7},{6,4},{7,5},{8,10},{9,11},{10,... | collective-permute-start | bytes 786440 | tf_op jit(solution)/shard_map/ppermute | solution.py:319
  34.4 11.2 %collective-permute-start.10 = (bf16[256,512]{1,0:T(8,128)(2,1)S(1)}, bf16[256,512]{1,0:T(8,128)(2,1)S(1)}, u32[]{:S(2)}, u32[]{:S(2)}) collective-permute-start(bf16[256,512]{1,0:T(8,128)(2,1)S(1)} %collective-permute-done.7.refs_6_), channel_id=1, source_target_pairs={{0,2},{1,3},{2,0},{3,1},{4,6},{5,7},{6,4},{7,5},{8,10},{9,11},{10,... | collective-permute-start | bytes 786440 | tf_op jit(solution)/shard_map/ppermute | solution.py:319
